TPU v7x, 256 devices: a whole 4x4x8 slice. The times are simulated.
256 devices in a mesh: seq: 64 (over y, z_lo, x), tp: 4 (over z_hi, core).
Axes of the slice: x: 4, y: 4, z: 8 (z_hi: 2, z_lo: 4; z = z_hi * 4 + z_lo), core: 2. Of those that a mesh axis runs over, the one named last changes fastest.
Arguments:
- hidden_in: bfloat16 [16384, 4096], P('seq', 'tp'), may hold values from -6 to 6
- order: int32 [16384], P('seq'), may hold values from 0 to 16383, as said below
- segment: int32 [16384], replicated, may hold values from 0 to 31, never falling along the last dimension, each value on 1 to 2048 neighbouring positions
- norm_gain: float32 [4096], replicated, may hold values from 0.1 to 1.9
- w_query: bfloat16 [4096, 2048], P('seq', 'tp')
- w_key: bfloat16 [4096, 512], P('seq', 'tp'), may hold values from -0.09375 to 0.09375
- w_value: bfloat16 [4096, 512], P('seq', 'tp'), may hold values from -0.09375 to 0.09375
- w_out: bfloat16 [2048, 4096], P('seq', 'tp'), may hold values from -0.5 to 0.5
Outputs:
- attn_out: bfloat16 [16384, 4096], P('seq', 'tp')
Inputs may be any that keep to these rules, and one draw needn't show every extreme that they name: order holds every position once; it is made of runs of 64 consecutive positions, each starting at a multiple of 64 and stored in rows that start at a multiple of 64. `segment`: never falls along positions.
All inputs are finite; a program needn't handle non-finite values.
Results may differ from a plain program's by a relative error of at most 0.014.
The roundings to bfloat16 on the way count: a program that leaves them out, or rounds other values in their place, can miss the bound.
Values may be sent and summed in bfloat16 or wider, within the bound.
No kernel may reach another device: no remote copies, remote signals or barrier semaphores. Data moves between devices by JAX's collectives and lax.ppermute only.
A program may use at most 128 MiB of HBM per device.

v0:
```python
import jax
import jax.numpy as jnp
from jax import lax
from jax.sharding import Mesh
from jax.sharding import PartitionSpec as P

HD = 128
SEQ = ("seq_0", "seq_1", "seq_2")
THETA = 500000.0
EPS = 1e-05


def sent_to_all(array, axis):
    copies = jnp.broadcast_to(array, (lax.axis_size(axis), *array.shape))
    return lax.all_to_all(copies, axis, split_axis=0, concat_axis=0, tiled=True)


def joined_along(blocks, dim):
    blocks = jnp.moveaxis(blocks, 0, dim)
    dims = blocks.shape
    return blocks.reshape(*dims[:dim], dims[dim] * dims[dim + 1], *dims[dim + 2 :])


def gather_directly(array, axis, dim):
    blocks = sent_to_all(array, axis)
    return joined_along(blocks, dim)


def side_by_side(arrays, axis, dim, along):
    widths = [a.shape[along] for a in arrays]
    both = jnp.concatenate(arrays, axis=along)
    filled = lax.all_gather(both, axis, axis=dim, tiled=True)
    return tuple(jnp.split(filled, [sum(widths[:k]) for k in range(1, len(widths))], axis=along))


def stacked_from(array, axes, sequence):
    blocks = array
    for k in sequence:
        blocks = lax.all_gather(blocks, axes[k])
    done = sequence[::-1]
    back = [done.index(k) for k in range(len(axes))]
    blocks = blocks.transpose(*back, *range(len(axes), blocks.ndim))
    return blocks.reshape(-1, *array.shape)


def gathered_by_axis(array, axes, sequence, dim):
    return joined_along(stacked_from(array, axes, sequence), dim)


def rotary(block, positions):
    head_dim = block.shape[-1]
    width = head_dim // 2
    frequency = THETA ** (-jnp.arange(width, dtype=jnp.float32) * 2.0 / head_dim)
    angle = positions.astype(jnp.float32)[:, None] * frequency[None, :]
    cosine = jnp.cos(angle)[:, None, :]
    sine = jnp.sin(angle)[:, None, :]
    first = block[..., :width]
    second = block[..., width:]
    return jnp.concatenate(
        [first * cosine - second * sine, second * cosine + first * sine], axis=-1
    )


def on_device(hidden_in, order, segment, norm_gain, w_query, w_key, w_value, w_out):
    rows = hidden_in.shape[0]
    whole = gather_directly(hidden_in, "tp", 1)
    wide = whole.astype(jnp.float32)
    mean_square = jnp.mean(wide * wide, axis=1, keepdims=True)
    normed = (wide * lax.rsqrt(mean_square + EPS) * norm_gain[None, :]).astype(jnp.bfloat16)
    pieces = side_by_side((w_query, w_key, w_value), SEQ, 0, 1)
    columns = normed
    query, key, value = tuple(
        (jnp.dot(columns, piece, preferred_element_type=jnp.float32) for piece in pieces)
    )
    heads_local = w_query.shape[1] // HD
    groups_local = w_key.shape[1] // HD
    group = heads_local // groups_local
    query = (rotary(query.reshape(rows, heads_local, HD), order) * HD ** (-0.5)).astype(
        jnp.bfloat16
    )
    query = query.reshape(rows, groups_local, group, HD)
    key = rotary(key.reshape(rows, groups_local, HD), order).astype(jnp.bfloat16)
    value = value.reshape(rows, groups_local, HD).astype(jnp.bfloat16)
    document = jnp.take(segment, order, axis=0)

    def attend(carry, block):
        key_block, value_block, key_order, key_document = block
        allowed = (key_order[None, :] <= order[:, None]) & (
            key_document[None, :] == document[:, None]
        )
        maximum, total, weighted = carry
        scores = jnp.einsum("rkgd,ckd->rkgc", query, key_block, preferred_element_type=jnp.float32)
        scores = jnp.where(allowed[:, None, None, :], scores, -jnp.inf)
        new_max = jnp.maximum(maximum, jnp.max(scores, axis=-1))
        anchor = jnp.where(new_max == -jnp.inf, 0.0, new_max)
        weights = jnp.exp(scores - anchor[..., None])
        shrink = jnp.exp(maximum - anchor)
        total = total * shrink + jnp.sum(weights, axis=-1)
        weighted = weighted * shrink[..., None] + jnp.einsum(
            "rkgc,ckd->rkgd",
            weights.astype(jnp.bfloat16),
            value_block,
            preferred_element_type=jnp.float32,
        )
        return (new_max, total, weighted)

    initial = (
        jnp.full((rows, groups_local, group), -jnp.inf, jnp.float32),
        jnp.zeros((rows, groups_local, group), jnp.float32),
        jnp.zeros((rows, groups_local, group, HD), jnp.float32),
    )
    carry = initial
    piece = (
        *side_by_side((key, value), SEQ, 0, 1),
        lax.all_gather(order, SEQ, axis=0, tiled=True),
        lax.all_gather(document, SEQ, axis=0, tiled=True),
    )
    count = piece[0].shape[0]
    stacked = tuple((member.reshape((count // 512, 512) + member.shape[1:]) for member in piece))
    carry, unused = lax.scan(lambda state, block: (attend(state, block), None), carry, stacked)
    maximum, total, weighted = carry
    mixed = (weighted / total[..., None]).reshape(rows, heads_local * HD).astype(jnp.bfloat16)
    every_head = gather_directly(mixed, "tp", 1)
    piece = gathered_by_axis(w_out, SEQ, (1, 0, 2), 0)
    columns = every_head
    result = jnp.dot(columns, piece, preferred_element_type=jnp.float32)
    return result.astype(jnp.bfloat16)


def solution(mesh):
    torus = Mesh(mesh.devices.reshape(4, 4, 4, mesh.shape["tp"]), ("seq_0", "seq_1", "seq_2", "tp"))
    placed = (
        P(SEQ, "tp"),
        P(SEQ),
        P(),
        P(),
        P(SEQ, "tp"),
        P(SEQ, "tp"),
        P(SEQ, "tp"),
        P(SEQ, "tp"),
    )
    return jax.shard_map(
        on_device, mesh=torus, in_specs=placed, out_specs=P(SEQ, "tp"), check_vma=False
    )
```

profile of v0, /device:TPU:1, one launch (start us, length us, event | category | flops | bytes accessed | tf_op | source)
XLA Modules:
  0.0 937.8 jit_solution(4467411417672132659)
XLA Ops:
  8.1 2.6 broadcast_in_dim.58
  10.8 9.9 %all-to-all-start = ((bf16[4,256,1024]{2,1,0:T(8,128)(2,1)}), bf16[4,256,1024]{2,1,0:T(8,128)(2,1)}, u32[]{:S(2)}, u32[]{:S(2)}) async-start(bf16[4,256,1024]{2,1,0:T(8,128)(2,1)} %broadcast_in_dim.58), calls=%async_computation | async-start | bytes 4194304 | tf_op jit(solution)/shard_map/all_to_all | solution.py:15
  20.7 67.4 %all-gather = bf16[128,1024]{1,0:T(8,128)(2,1)} all-gather(bf16[32,1024]{1,0:T(8,128)(2,1)S(1)} %copy-done.5), channel_id=2, replica_groups=mesh['seq_0'=4,'seq_1'=4,'seq_2'=4,'tp'=4] {'seq_1'}, dimensions={0}, use_global_device_ids=true | all-gather | bytes 327680 | tf_op jit(solution)/shard_map/all_gather | solution.py:39
  88.3 1.7 gather_fusion
  90.0 2.9 copy.37
  93.5 1.7 fusion.21
  95.2 248.8 %all-gather.10.cloned.1.call-done = bf16[4096,768]{1,0:T(8,128)(2,1)} async-done(((bf16[64,768]{1,0:T(8,128)(2,1)}), bf16[4096,768]{1,0:T(8,128)(2,1)}) %all-gather.10.cloned.1.call-update) | async-done | bytes 6291472 | tf_op jit(solution)/shard_map/all_gather | solution.py:32
  344.0 2.4 convolution_bitcast_fusion.1
  346.7 2.4 fusion.22
  349.9 159.7 %all-gather.4 = s32[64,1,256]{2,1,0:T(1,128)S(1)} all-gather(s32[1,1,256]{2,1,0:T(1,128)S(1)} %bitcast.141), channel_id=1, replica_groups=mesh['seq_0'=4,'seq_1'=4,'seq_2'=4,'tp'=4] {'seq_0','seq_1','seq_2'}, dimensions={0}, use_global_device_ids=true | all-gather | bytes 66560 | tf_op jit(solution)/shard_map/all_gather | solution.py:116
  509.8 155.2 %all-gather.3 = s32[64,1,256]{2,1,0:T(1,128)S(1)} all-gather(s32[1,1,256]{2,1,0:T(1,128)S(1)} %bitcast.140), channel_id=1, replica_groups=mesh['seq_0'=4,'seq_1'=4,'seq_2'=4,'tp'=4] {'seq_0','seq_1','seq_2'}, dimensions={0}, use_global_device_ids=true | all-gather | bytes 66560 | tf_op jit(solution)/shard_map/all_gather | solution.py:115
  665.6 1.7 multiply_convert_fusion
  667.3 4.5 slice_bitcast_fusion
  671.8 6.6 copy.39
  678.4 3.4 fusion.36
  682.2 5.1 fusion.34
  687.3 2.5 copy.52
  689.8 6.4 copy.48
  696.2 117.0 %while.15 = (s32[]{:T(128)}, f32[256,1,4]{0,2,1:T(4,128)S(1)}, f32[256,1,4]{0,2,1:T(4,128)S(1)}, f32[256,1,4,128]{0,3,2,1:T(8,128)S(1)}, s32[32,512]{1,0:T(8,128...) while((s32[]{:T(128)}, f32[256,1,4]{0,2,1:T(4,128)S(1)}, ...), condition=%wide.region_4.5_spmd.clone, body=%wide.region_1.4_spmd.clone.sunk | while | flops 273428480 | bytes 8476829 | solution.py:120
  698.2 1.6 fusion.56
  705.6 1.6 fusion.56
  709.2 1.6 fusion.56
  712.9 1.6 fusion.56
  720.2 1.6 fusion.56
  723.8 1.6 fusion.56
  727.5 1.6 fusion.56
  734.8 1.6 fusion.56
  738.5 1.6 fusion.56
  742.1 1.6 fusion.56
  749.4 1.6 fusion.56
  753.1 1.6 fusion.56
  756.8 1.6 fusion.56
  764.1 1.6 fusion.56
  767.8 1.6 fusion.56
  771.4 1.6 fusion.56
  775.1 1.6 fusion.56
  778.7 1.6 fusion.56
  782.4 1.6 fusion.56
  786.1 1.6 fusion.56
  789.7 1.6 fusion.56
  797.0 1.6 fusion.56
  800.7 1.6 fusion.56
  804.4 1.6 fusion.56
  811.7 1.6 fusion.56
  814.4 95.3 %all-to-all-start.1 = ((bf16[4,256,512]{1,2,0:T(8,128)(2,1)}), bf16[4,256,512]{1,2,0:T(8,128)(2,1)S(1)}, u32[]{:S(2)}, u32[]{:S(2)}) async-start(bf16[4,256,512]{1,2,0:T(8,128)(2,1)} %broadcast_in_dim.59), calls=%async_computation.1 | async-start | bytes 2097152 | tf_op jit(solution)/shard_map/all_to_all | solution.py:15
  909.7 5.0 copy.44
  914.7 12.4 %all-to-all-done.1 = bf16[4,256,512]{1,2,0:T(8,128)(2,1)S(1)} async-done(((bf16[4,256,512]{1,2,0:T(8,128)(2,1)}), bf16[4,256,512]{1,2,0:T(8,128)(2,1)S(1)}, u32[]{:S(2)}, u32[]{:S(2)}) %all-to-all-start.1) | async-done | bytes 1048608 | tf_op jit(solution)/shard_map/all_to_all | solution.py:15
  927.0 4.3 convolution_convert_fusion
  (310 shorter events, 80.8 us)
Async XLA Ops:
  6.5 81.7 %copy-start = (s32[16384]{0:T(1024)S(1)}, s32[16384]{0:T(1024)}, u32[]{:S(2)}) copy-start(s32[16384]{0:T(1024)} %param.12) | copy-start | bytes 196612
  6.5 14.2 %copy-start.5 = (bf16[32,1024]{1,0:T(8,128)(2,1)S(1)}, bf16[32,1024]{1,0:T(8,128)(2,1)}, u32[]{:S(2)}) copy-start(bf16[32,1024]{1,0:T(8,128)(2,1)} %param.17) | copy-start | bytes 196612
  6.5 81.7 %copy-start.3 = (s32[256]{0:T(256)S(1)}, s32[256]{0:T(256)}, u32[]{:S(2)}) copy-start(s32[256]{0:T(256)} %param.11) | copy-start | bytes 3076
  6.5 337.4 %all-gather.10.cloned.1.call-start = ((), (), s32[]{:S(2)}) async-start(), calls=%async_computation.2 | async-start | bytes 6389760 | tf_op jit(solution)/shard_map/all_gather | solution.py:32
  10.8 79.2 %all-to-all-start = ((bf16[4,256,1024]{2,1,0:T(8,128)(2,1)}), bf16[4,256,1024]{2,1,0:T(8,128)(2,1)}, u32[]{:S(2)}, u32[]{:S(2)}) async-start(bf16[4,256,1024]{2,1,0:T(8,128)(2,1)} %broadcast_in_dim.58), calls=%async_computation | async-start | bytes 4194304 | tf_op jit(solution)/shard_map/all_to_all | solution.py:15
  20.7 72.8 %copy-start.4 = (f32[4096]{0:T(1024)S(1)}, f32[4096]{0:T(1024)}, u32[]{:S(2)}) copy-start(f32[4096]{0:T(1024)} %param.13) | copy-start | bytes 49156
  20.7 644.9 %all-gather.14.cloned.1.call-start = ((), (), s32[]{:S(2)}) async-start(), calls=%async_computation.4 | async-start | bytes 1310720 | tf_op jit(solution)/shard_map/all_gather | solution.py:39
  88.2 594.0 %all-gather.12.cloned.1.call-start = ((), (), s32[]{:S(2)}) async-start(), calls=%async_computation.3 | async-start | bytes 8519680 | tf_op jit(solution)/shard_map/all_gather | solution.py:32
  349.8 559.8 %all-gather.16.cloned.1.call-start = ((), (), s32[]{:S(2)}) async-start(), calls=%async_computation.5 | async-start | bytes 5242880 | tf_op jit(solution)/shard_map/all_gather | solution.py:39
  671.8 6.6 copy-start.2
  814.4 112.7 %all-to-all-start.1 = ((bf16[4,256,512]{1,2,0:T(8,128)(2,1)}), bf16[4,256,512]{1,2,0:T(8,128)(2,1)S(1)}, u32[]{:S(2)}, u32[]{:S(2)}) async-start(bf16[4,256,512]{1,2,0:T(8,128)(2,1)} %broadcast_in_dim.59), calls=%async_computation.1 | async-start | bytes 2097152 | tf_op jit(solution)/shard_map/all_to_all | solution.py:15
  909.7 21.6 %copy-start.1 = (s32[16384]{0:T(1024)S(1)}, s32[16384]{0:T(1024)}, u32[]{:S(2)}) copy-start(s32[16384]{0:T(1024)} %param.12) | copy-start | bytes 196612
Sparse Core Ops, SparseCore 0:
  9.1 334.8 all-gather.9
  345.8 63.5 all-gather.13
  411.1 267.4 all-gather.11
  680.2 121.1 all-gather.15
where the time goes:
time: 940 us; the launch traced here: 938 us
  blocking collectives  382 us (41%)
  waiting for transfers between devices  261 us (28%)
  matrix products  106 us (11%)
  starting transfers between devices  105 us (11%)
  local copies, waits for them, and re-layouts  39.1 us (4%)
  other arithmetic  27.8 us (3%)
  between operations  13.3 us (1%)
    all_gather x2, waiting for transfers between devices, side_by_side(): filled = lax.all_gather(both, axis, axis=dim, tiled=True)  249 us
    all_gather x1, blocking collectives, on_device(): lax.all_gather(document, SEQ, axis=0, tiled=True)  160 us
    all_gather x1, blocking collectives, on_device(): lax.all_gather(order, SEQ, axis=0, tiled=True)  155 us
    all_to_all x2, starting transfers between devices, sent_to_all(): return lax.all_to_all(copies, axis, split_axis=0, concat_axis=0, tiled=True)  105 us
    all_gather x1, blocking collectives, stacked_from(): blocks = lax.all_gather(blocks, axes[k])  67.4 us
    dot_general x32, matrix products, attend(): jnp.einsum('rkgc,ckd->rkgd', weights.astype(jnp.bfloat16), value_block, p...  50.5 us
    dot_general x32, matrix products, attend(): jnp.einsum('rkgd,ckd->rkgc', query, key_block, preferred_element_type=jnp...  43.4 us
  transfers between devices with their start and end apart: 6, of which 2 were waited for; matrix products, arithmetic and copies ran while one was open for 18% of the time, Pallas kernels for 0%

commit v1 on v0

--- a/solution.py
+++ b/solution.py
@@ -112,7 +112,7 @@
     carry = initial
     piece = (
         *side_by_side((key, value), SEQ, 0, 1),
-        lax.all_gather(order, SEQ, axis=0, tiled=True),
+        jnp.concatenate(lax.all_to_all(jnp.stack([order] * lax.axis_size(SEQ)), SEQ, 0, 0), axis=0),
         lax.all_gather(document, SEQ, axis=0, tiled=True),
     )
     count = piece[0].shape[0]

time: 940 us -> 886 us (0.943)
  blocking collectives: 382 us -> 228 us
  waiting for transfers between devices: 261 us -> 411 us
  starting transfers between devices: 105 us -> 55.6 us
    all_gather x1 -> x0, blocking collectives: 155 us -> none  [on_device(): lax.all_gather(order, SEQ, axis=0, tiled=True)]
    all_gather x2, waiting for transfers between devices: 249 us -> 391 us  [side_by_side(): filled = lax.all_gather(both, axis, axis=dim, tiled=True)]
    all_to_all x2, starting transfers between devices: 105 us -> 47.3 us  [sent_to_all(): return lax.all_to_all(copies, axis, split_axis=0, concat_axis=0, tiled=True)]
  transfers between devices with their start and end apart: 6 -> 7, of which waited for: 2 -> 3; matrix products, arithmetic and copies ran while one was open for 18% -> 19% of each run, Pallas kernels for 0% -> 0%
where the time goes in v1:
time: 886 us; the launch traced here: 884 us
  waiting for transfers between devices  411 us (46%)
  blocking collectives  228 us (26%)
  matrix products  106 us (12%)
  starting transfers between devices  55.6 us (6%)
  local copies, waits for them, and re-layouts  39.7 us (4%)
  other arithmetic  27.8 us (3%)
  between operations  13.4 us (2%)
    all_gather x2, waiting for transfers between devices, side_by_side(): filled = lax.all_gather(both, axis, axis=dim, tiled=True)  391 us
    all_gather x1, blocking collectives, on_device(): lax.all_gather(document, SEQ, axis=0, tiled=True)  161 us
    all_gather x1, blocking collectives, stacked_from(): blocks = lax.all_gather(blocks, axes[k])  67.4 us
    dot_general x32, matrix products, attend(): jnp.einsum('rkgc,ckd->rkgd', weights.astype(jnp.bfloat16), value_block, p...  50.5 us
    all_to_all x2, starting transfers between devices, sent_to_all(): return lax.all_to_all(copies, axis, split_axis=0, concat_axis=0, tiled=True)  47.3 us
    dot_general x32, matrix products, attend(): jnp.einsum('rkgd,ckd->rkgc', query, key_block, preferred_element_type=jnp...  43.4 us
    all_to_all x2, waiting for transfers between devices, sent_to_all(): return lax.all_to_all(copies, axis, split_axis=0, concat_axis=0, tiled=True)  19.2 us
  transfers between devices with their start and end apart: 7, of which 3 were waited for; matrix products, arithmetic and copies ran while one was open for 19% of the time, Pallas kernels for 0%

profile of v1, /device:TPU:1, one launch (start us, length us, event | category | flops | bytes accessed | tf_op | source)
XLA Modules:
  0.0 883.7 jit_solution(17115614871665205951)
XLA Ops:
  8.1 2.6 broadcast_in_dim.58
  10.8 9.9 %all-to-all-start.1 = ((bf16[4,256,1024]{2,1,0:T(8,128)(2,1)}), bf16[4,256,1024]{2,1,0:T(8,128)(2,1)}, u32[]{:S(2)}, u32[]{:S(2)}) async-start(bf16[4,256,1024]{2,1,0:T(8,128)(2,1)} %broadcast_in_dim.58), calls=%async_computation.1 | async-start | bytes 4194304 | tf_op jit(solution)/shard_map/all_to_all | solution.py:15
  20.7 67.4 %all-gather = bf16[128,1024]{1,0:T(8,128)(2,1)} all-gather(bf16[32,1024]{1,0:T(8,128)(2,1)S(1)} %copy-done.5), channel_id=2, replica_groups=mesh['seq_0'=4,'seq_1'=4,'seq_2'=4,'tp'=4] {'seq_1'}, dimensions={0}, use_global_device_ids=true | all-gather | bytes 327680 | tf_op jit(solution)/shard_map/all_gather | solution.py:39
  88.3 1.7 gather_fusion
  90.0 2.9 copy.37
  93.5 1.7 fusion.21
  95.2 248.7 %all-gather.9.cloned.1.call-done = bf16[4096,768]{1,0:T(8,128)(2,1)} async-done(((bf16[64,768]{1,0:T(8,128)(2,1)}), bf16[4096,768]{1,0:T(8,128)(2,1)}) %all-gather.9.cloned.1.call-update) | async-done | bytes 6291472 | tf_op jit(solution)/shard_map/all_gather | solution.py:32
  343.9 2.4 convolution_bitcast_fusion.1
  346.7 2.4 fusion.22
  350.5 8.3 all-to-all-start
  358.9 160.5 %all-gather.3 = s32[64,1,256]{2,1,0:T(1,128)S(1)} all-gather(s32[1,1,256]{2,1,0:T(1,128)S(1)} %bitcast.139), channel_id=1, replica_groups=mesh['seq_0'=4,'seq_1'=4,'seq_2'=4,'tp'=4] {'seq_0','seq_1','seq_2'}, dimensions={0}, use_global_device_ids=true | all-gather | bytes 66560 | tf_op jit(solution)/shard_map/all_gather | solution.py:116
  520.2 1.7 multiply_convert_fusion
  521.9 4.5 slice_bitcast_fusion
  526.4 6.5 copy.39
  532.9 3.5 fusion.36
  536.7 142.6 %all-gather.11.cloned.1.call-done = bf16[16384,2,128]{0,2,1:T(8,128)(2,1)} async-done(((bf16[256,2,128]{0,2,1:T(8,128)(2,1)}), bf16[16384,2,128]{0,2,1:T(8,128)(2,1)}) %all-gather.11.cloned.1.call-update) | async-done | bytes 8388624 | tf_op jit(solution)/shard_map/all_gather | solution.py:32
  679.3 5.1 fusion.34
  684.4 2.5 copy.52
  686.9 6.4 copy.48
  693.3 117.1 %while.15 = (s32[]{:T(128)}, f32[256,1,4]{0,2,1:T(4,128)S(1)}, f32[256,1,4]{0,2,1:T(4,128)S(1)}, f32[256,1,4,128]{0,3,2,1:T(8,128)S(1)}, s32[32,512]{1,0:T(8,128...) while((s32[]{:T(128)}, f32[256,1,4]{0,2,1:T(4,128)S(1)}, ...), condition=%wide.region_4.5_spmd.clone, body=%wide.region_1.4_spmd.clone.sunk | while | flops 273428480 | bytes 8476829 | solution.py:120
  695.3 1.6 fusion.56
  699.0 1.6 fusion.56
  702.6 1.6 fusion.56
  709.9 1.6 fusion.56
  713.6 1.6 fusion.56
  717.3 1.6 fusion.56
  724.6 1.6 fusion.56
  731.9 1.6 fusion.56
  735.6 1.6 fusion.56
  739.2 1.6 fusion.56
  742.9 1.6 fusion.56
  746.6 1.6 fusion.56
  750.2 1.6 fusion.56
  753.9 1.6 fusion.56
  761.2 1.6 fusion.56
  764.9 1.6 fusion.56
  768.5 1.6 fusion.56
  775.8 1.6 fusion.56
  779.5 1.6 fusion.56
  783.1 1.6 fusion.56
  790.5 1.6 fusion.56
  794.1 1.6 fusion.56
  797.8 1.6 fusion.56
  808.7 1.6 fusion.56
  811.5 37.3 %all-to-all-start.2 = ((bf16[4,256,512]{1,2,0:T(8,128)(2,1)}), bf16[4,256,512]{1,2,0:T(8,128)(2,1)S(1)}, u32[]{:S(2)}, u32[]{:S(2)}) async-start(bf16[4,256,512]{1,2,0:T(8,128)(2,1)} %broadcast_in_dim.59), calls=%async_computation.2 | async-start | bytes 2097152 | tf_op jit(solution)/shard_map/all_to_all | solution.py:15
  848.8 5.0 copy.44
  853.8 19.2 %all-to-all-done.2 = bf16[4,256,512]{1,2,0:T(8,128)(2,1)S(1)} async-done(((bf16[4,256,512]{1,2,0:T(8,128)(2,1)}), bf16[4,256,512]{1,2,0:T(8,128)(2,1)S(1)}, u32[]{:S(2)}, u32[]{:S(2)}) %all-to-all-start.2) | async-done | bytes 1048608 | tf_op jit(solution)/shard_map/all_to_all | solution.py:15
  872.9 4.3 convolution_convert_fusion
  (312 shorter events, 83.1 us)
Async XLA Ops:
  6.5 81.7 %copy-start = (s32[16384]{0:T(1024)S(1)}, s32[16384]{0:T(1024)}, u32[]{:S(2)}) copy-start(s32[16384]{0:T(1024)} %param.12) | copy-start | bytes 196612
  6.5 14.2 %copy-start.5 = (bf16[32,1024]{1,0:T(8,128)(2,1)S(1)}, bf16[32,1024]{1,0:T(8,128)(2,1)}, u32[]{:S(2)}) copy-start(bf16[32,1024]{1,0:T(8,128)(2,1)} %param.17) | copy-start | bytes 196612
  6.5 81.7 %copy-start.3 = (s32[256]{0:T(256)S(1)}, s32[256]{0:T(256)}, u32[]{:S(2)}) copy-start(s32[256]{0:T(256)} %param.11) | copy-start | bytes 3076
  6.5 337.4 %all-gather.9.cloned.1.call-start = ((), (), s32[]{:S(2)}) async-start(), calls=%async_computation.3 | async-start | bytes 6389760 | tf_op jit(solution)/shard_map/all_gather | solution.py:32
  10.8 79.3 %all-to-all-start.1 = ((bf16[4,256,1024]{2,1,0:T(8,128)(2,1)}), bf16[4,256,1024]{2,1,0:T(8,128)(2,1)}, u32[]{:S(2)}, u32[]{:S(2)}) async-start(bf16[4,256,1024]{2,1,0:T(8,128)(2,1)} %broadcast_in_dim.58), calls=%async_computation.1 | async-start | bytes 4194304 | tf_op jit(solution)/shard_map/all_to_all | solution.py:15
  20.7 72.8 %copy-start.4 = (f32[4096]{0:T(1024)S(1)}, f32[4096]{0:T(1024)}, u32[]{:S(2)}) copy-start(f32[4096]{0:T(1024)} %param.13) | copy-start | bytes 49156
  20.7 499.4 %all-gather.13.cloned.1.call-start = ((), (), s32[]{:S(2)}) async-start(), calls=%async_computation.5 | async-start | bytes 1310720 | tf_op jit(solution)/shard_map/all_gather | solution.py:39
  88.2 591.1 %all-gather.11.cloned.1.call-start = ((), (), s32[]{:S(2)}) async-start(), calls=%async_computation.4 | async-start | bytes 8519680 | tf_op jit(solution)/shard_map/all_gather | solution.py:32
  350.5 169.4 %all-to-all-start = ((s32[64,1,256]{2,1,0:T(1,128)}), s32[64,1,256]{2,1,0:T(1,128)S(1)}, u32[]{:S(2)}, u32[]{:S(2)}) async-start(s32[64,1,256]{2,1,0:T(1,128)} %stack.2), calls=%async_computation | async-start | bytes 131072 | tf_op jit(solution)/shard_map/all_to_all | solution.py:115
  358.8 490.0 %all-gather.15.cloned.1.call-start = ((), (), s32[]{:S(2)}) async-start(), calls=%async_computation.6 | async-start | bytes 5242880 | tf_op jit(solution)/shard_map/all_gather | solution.py:39
  526.4 6.5 copy-start.2
  811.5 61.5 %all-to-all-start.2 = ((bf16[4,256,512]{1,2,0:T(8,128)(2,1)}), bf16[4,256,512]{1,2,0:T(8,128)(2,1)S(1)}, u32[]{:S(2)}, u32[]{:S(2)}) async-start(bf16[4,256,512]{1,2,0:T(8,128)(2,1)} %broadcast_in_dim.59), calls=%async_computation.2 | async-start | bytes 2097152 | tf_op jit(solution)/shard_map/all_to_all | solution.py:15
  848.8 28.4 %copy-start.1 = (s32[16384]{0:T(1024)S(1)}, s32[16384]{0:T(1024)}, u32[]{:S(2)}) copy-start(s32[16384]{0:T(1024)} %param.12) | copy-start | bytes 196612
Sparse Core Ops, SparseCore 0:
  9.1 334.7 all-gather.8
  345.7 63.8 all-gather.12
  411.4 267.9 all-gather.10
  681.0 80.5 all-gather.14
